TPU v7x, 8 devices: a whole 2x2x1 slice. The times are simulated.
8 devices in a mesh: fsdp: 8 (over z, y, x, core).
Axes of the slice: x: 2, y: 2, z: 1, core: 2. Of those that a mesh axis runs over, the one named last changes fastest.
Arguments:
- x_in: bfloat16 [8, 768, 1024], P('fsdp')
- positions: int32 [768], replicated
- grad_out: bfloat16 [8, 768, 1024], P('fsdp')
- ln_gamma_1: float32 [1024], P('fsdp')
- w_q_1: bfloat16 [1024, 2048], P('fsdp')
- w_k_1: bfloat16 [1024, 1024], P('fsdp')
- w_v_1: bfloat16 [1024, 1024], P('fsdp')
- w_o_1: bfloat16 [2048, 1024], P('fsdp')
- w_gate_1: bfloat16 [1024, 3072], P('fsdp')
- w_up_1: bfloat16 [1024, 3072], P('fsdp')
- w_down_1: bfloat16 [3072, 1024], P('fsdp')
- q_norm_1: float32 [2048], P('fsdp')
- k_norm_1: float32 [1024], P('fsdp')
- ln_gamma_2: float32 [1024], P('fsdp')
- w_q_2: bfloat16 [1024, 2048], P('fsdp')
- w_k_2: bfloat16 [1024, 1024], P('fsdp')
- w_v_2: bfloat16 [1024, 1024], P('fsdp')
- w_o_2: bfloat16 [2048, 1024], P('fsdp')
- w_gate_2: bfloat16 [1024, 3072], P('fsdp')
- w_up_2: bfloat16 [1024, 3072], P('fsdp')
- w_down_2: bfloat16 [3072, 1024], P('fsdp')
- q_norm_2: float32 [2048], P('fsdp')
- k_norm_2: float32 [1024], P('fsdp')
Outputs:
- output 1: bfloat16 [8, 768, 1024], P('fsdp')
- output 2: bfloat16 [8, 768, 1024], P('fsdp')
- output 3: float32 [1024], P('fsdp')
- output 4: float32 [1024, 2048], P('fsdp')
- output 5: float32 [1024, 1024], P('fsdp')
- output 6: float32 [1024, 1024], P('fsdp')
- output 7: float32 [2048, 1024], P('fsdp')
- output 8: float32 [1024, 3072], P('fsdp')
- output 9: float32 [1024, 3072], P('fsdp')
- output 10: float32 [3072, 1024], P('fsdp')
- output 11: float32 [2048], P('fsdp')
- output 12: float32 [1024], P('fsdp')
- output 13: float32 [1024], P('fsdp')
- output 14: float32 [1024, 2048], P('fsdp')
- output 15: float32 [1024, 1024], P('fsdp')
- output 16: float32 [1024, 1024], P('fsdp')
- output 17: float32 [2048, 1024], P('fsdp')
- output 18: float32 [1024, 3072], P('fsdp')
- output 19: float32 [1024, 3072], P('fsdp')
- output 20: float32 [3072, 1024], P('fsdp')
- output 21: float32 [2048], P('fsdp')
- output 22: float32 [1024], P('fsdp')
All inputs are finite; a program needn't handle non-finite values.
Results may differ from a plain program's by a relative error of at most 0.0186895.
Values are sent between devices in bfloat16 or wider.
A program may use at most 1 GiB of HBM per device.

v0:
```python
import functools
import jax
import jax.numpy as jnp
from jax import lax
from jax.sharding import PartitionSpec as P, NamedSharding

HEAD_DIM = 128
EPSILON = 1e-5
ROPE_THETA = 7.5e7
FSDP_AXIS = 'fsdp'


def layer_norm32(values, weight):
    row_mean = jnp.mean(values, axis=-1, keepdims=True)
    centered = values - row_mean
    variance = jnp.mean(centered * centered, axis=-1, keepdims=True)
    return centered * lax.rsqrt(variance + EPSILON) * weight


def rope_tables(positions):
    inv_freq = ROPE_THETA ** (-jnp.arange(0, HEAD_DIM, 2, dtype=jnp.float32) / HEAD_DIM)
    angles = positions.astype(jnp.float32)[:, None] * inv_freq[None, :]
    return jnp.cos(angles), jnp.sin(angles)


def apply_rope(values, cos_tab, sin_tab):
    pair_view = values.reshape(values.shape[:-1] + (HEAD_DIM // 2, 2))
    even_part = pair_view[..., 0]
    odd_part = pair_view[..., 1]
    cos_b = cos_tab[:, None, :]
    sin_b = sin_tab[:, None, :]
    rotated = jnp.stack([even_part * cos_b - odd_part * sin_b, even_part * sin_b + odd_part * cos_b], axis=-1)
    return rotated.reshape(values.shape)


def attention_core(q_raw, k_raw, v_heads, q_norm, k_norm, cos_tab, sin_tab):
    batch_len, seq_len, n_heads = q_raw.shape[0], q_raw.shape[1], q_raw.shape[2]
    n_kv = k_raw.shape[2]
    q_rot = apply_rope(layer_norm32(q_raw, q_norm), cos_tab, sin_tab).astype(jnp.bfloat16)
    k_rot = apply_rope(layer_norm32(k_raw, k_norm), cos_tab, sin_tab).astype(jnp.bfloat16)
    q_grp = q_rot.reshape(batch_len, seq_len, n_kv, n_heads // n_kv, HEAD_DIM)
    scores = jnp.einsum('bqkgd,bskd->bkgqs', q_grp, k_rot, preferred_element_type=jnp.float32) * HEAD_DIM ** -0.5
    causal = jnp.arange(seq_len)[:, None] >= jnp.arange(seq_len)[None, :]
    attn_prob = jax.nn.softmax(jnp.where(causal, scores, -1e30), axis=-1).astype(jnp.bfloat16)
    context = jnp.einsum('bkgqs,bskd->bqkgd', attn_prob, v_heads, preferred_element_type=jnp.float32)
    return context.astype(jnp.bfloat16).reshape(batch_len, seq_len, n_heads * HEAD_DIM)


def swiglu(gate_proj, up_proj):
    return jax.nn.silu(gate_proj) * up_proj


def layer_forward(stream, params, cos_tab, sin_tab):
    ln_gamma, w_q, w_k, w_v, w_o, w_gate, w_up, w_down, q_norm, k_norm = params
    lead_shape = stream.shape[:-1]
    n_heads = w_q.shape[1] // HEAD_DIM
    n_kv = w_k.shape[1] // HEAD_DIM
    x_f32 = stream.astype(jnp.float32)
    normed = layer_norm32(x_f32, ln_gamma).astype(jnp.bfloat16)
    q_raw = jnp.dot(normed, w_q, preferred_element_type=jnp.float32).reshape(lead_shape + (n_heads, HEAD_DIM))
    k_raw = jnp.dot(normed, w_k, preferred_element_type=jnp.float32).reshape(lead_shape + (n_kv, HEAD_DIM))
    v_heads = jnp.dot(normed, w_v, preferred_element_type=jnp.float32).astype(jnp.bfloat16).reshape(lead_shape + (n_kv, HEAD_DIM))
    attn_out = attention_core(q_raw, k_raw, v_heads, q_norm.reshape(n_heads, HEAD_DIM), k_norm.reshape(n_kv, HEAD_DIM), cos_tab, sin_tab)
    gate_proj = jnp.dot(normed, w_gate, preferred_element_type=jnp.float32)
    up_proj = jnp.dot(normed, w_up, preferred_element_type=jnp.float32)
    hidden = swiglu(gate_proj, up_proj).astype(jnp.bfloat16)
    layer_sum = x_f32 + jnp.dot(attn_out, w_o, preferred_element_type=jnp.float32) + jnp.dot(hidden, w_down, preferred_element_type=jnp.float32)
    saved_acts = (stream, normed, q_raw, k_raw, v_heads, attn_out, gate_proj, up_proj, hidden)
    return layer_sum.astype(jnp.bfloat16), saved_acts


def layer_backward(grad_y, saved_acts, params, cos_tab, sin_tab):
    ln_gamma, w_q, w_k, w_v, w_o, w_gate, w_up, w_down, q_norm, k_norm = params
    stream, normed, q_raw, k_raw, v_heads, attn_out, gate_proj, up_proj, hidden = saved_acts
    lead_shape = stream.shape[:-1]
    n_heads = q_raw.shape[-2]
    n_kv = k_raw.shape[-2]
    g_w_down = jnp.einsum('bsf,bsd->fd', hidden, grad_y, preferred_element_type=jnp.float32)
    g_w_o = jnp.einsum('bsn,bsd->nd', attn_out, grad_y, preferred_element_type=jnp.float32)
    d_hidden = jnp.einsum('bsd,fd->bsf', grad_y, w_down, preferred_element_type=jnp.float32)
    swiglu_vjp = jax.vjp(swiglu, gate_proj, up_proj)[1]
    d_gate, d_up = swiglu_vjp(d_hidden)
    d_gate = d_gate.astype(jnp.bfloat16)
    d_up = d_up.astype(jnp.bfloat16)
    g_w_gate = jnp.einsum('bsd,bsf->df', normed, d_gate, preferred_element_type=jnp.float32)
    g_w_up = jnp.einsum('bsd,bsf->df', normed, d_up, preferred_element_type=jnp.float32)
    d_attn = jnp.einsum('bsd,nd->bsn', grad_y, w_o, preferred_element_type=jnp.float32).astype(jnp.bfloat16)
    core_fn = functools.partial(attention_core, cos_tab=cos_tab, sin_tab=sin_tab)
    core_vjp = jax.vjp(core_fn, q_raw, k_raw, v_heads, q_norm.reshape(n_heads, HEAD_DIM), k_norm.reshape(n_kv, HEAD_DIM))[1]
    d_qraw, d_kraw, d_vheads, g_q_norm, g_k_norm = core_vjp(d_attn)
    d_q = d_qraw.astype(jnp.bfloat16).reshape(lead_shape + (n_heads * HEAD_DIM,))
    d_k = d_kraw.astype(jnp.bfloat16).reshape(lead_shape + (n_kv * HEAD_DIM,))
    d_v = d_vheads.reshape(lead_shape + (n_kv * HEAD_DIM,))
    g_w_q = jnp.einsum('bsd,bsn->dn', normed, d_q, preferred_element_type=jnp.float32)
    g_w_k = jnp.einsum('bsd,bsn->dn', normed, d_k, preferred_element_type=jnp.float32)
    g_w_v = jnp.einsum('bsd,bsn->dn', normed, d_v, preferred_element_type=jnp.float32)
    d_normed = (jnp.einsum('bsf,df->bsd', d_gate, w_gate, preferred_element_type=jnp.float32)
                + jnp.einsum('bsf,df->bsd', d_up, w_up, preferred_element_type=jnp.float32)
                + jnp.einsum('bsn,dn->bsd', d_q, w_q, preferred_element_type=jnp.float32)
                + jnp.einsum('bsn,dn->bsd', d_k, w_k, preferred_element_type=jnp.float32)
                + jnp.einsum('bsn,dn->bsd', d_v, w_v, preferred_element_type=jnp.float32))
    norm_vjp = jax.vjp(layer_norm32, stream.astype(jnp.float32), ln_gamma)[1]
    d_stream, g_ln_gamma = norm_vjp(d_normed)
    grad_x = (grad_y.astype(jnp.float32) + d_stream).astype(jnp.bfloat16)
    grads = (g_ln_gamma, g_w_q, g_w_k, g_w_v, g_w_o, g_w_gate, g_w_up, g_w_down, g_q_norm.reshape(-1), g_k_norm.reshape(-1))
    return grad_x, grads


def gather_full(shards):
    return tuple(lax.all_gather(param_piece, FSDP_AXIS, axis=0, tiled=True) for param_piece in shards)


def reduce_shards(grads):
    return tuple(lax.psum_scatter(part_grad, FSDP_AXIS, scatter_dimension=0, tiled=True) for part_grad in grads)


def layer_specs():
    vector_spec = P(FSDP_AXIS)
    matrix_spec = P(FSDP_AXIS, None)
    return (vector_spec,) + (matrix_spec,) * 7 + (vector_spec, vector_spec)


def solution(mesh):
    act_spec = P(FSDP_AXIS, None, None)
    param_spec = layer_specs()
    in_specs = (act_spec, P(), act_spec) + param_spec + param_spec
    out_specs = (act_spec, act_spec) + param_spec + param_spec

    def body(x_in, positions, grad_out, *shards):
        cos_tab, sin_tab = rope_tables(positions)
        half_count = len(shards) // 2
        layer_shards = [shards[:half_count], shards[half_count:]]
        stream = x_in
        saved_list = []
        for layer_params in layer_shards:
            full_params = gather_full(layer_params)
            stream, saved_acts = layer_forward(stream, full_params, cos_tab, sin_tab)
            saved_list.append(saved_acts)
        grad_stream = grad_out
        grad_parts = [None, None]
        for layer_index in (1, 0):
            own_shards, grad_stream, stream = lax.optimization_barrier((layer_shards[layer_index], grad_stream, stream))
            full_params = gather_full(own_shards)
            grad_stream, grads = layer_backward(grad_stream, saved_list[layer_index], full_params, cos_tab, sin_tab)
            grad_parts[layer_index] = reduce_shards(grads)
        return (stream, grad_stream) + grad_parts[0] + grad_parts[1]

    return jax.shard_map(body, mesh=mesh, in_specs=in_specs, out_specs=out_specs, check_vma=False)
```

profile of v0, /device:TPU:0, one launch (start us, length us, event | category | flops | bytes accessed | tf_op | source)
XLA Modules:
  0.0 2205.3 jit_solution(12943741636307313820)
XLA Ops:
  209.5 18.2 fusion.22
  227.7 16.3 fusion.18
  244.0 19.0 fusion.88
  431.9 17.9 fusion.23
  484.0 16.2 fusion.19
  500.2 18.7 fusion.91
  610.2 18.5 fusion.20
  628.7 16.5 fusion.138
  657.7 24.2 %fusion.8 = (f32[8,2,768]{2,1,0:T(2,128)S(1)}, bf16[8,2,768,768]{2,3,1,0:T(8,128)(2,1)}) fusion(f32[8,2,768]{2,1,0:T(2,128)S(1)} %multiply_divide_fusion.1, f32[8,2,768]{2,1,0:T(2,128)S(1)} %get-tuple-element.128, f32[8,768,768,2]{2,1,3,0:T(8,128)} %get-tuple-element.129, pred[768,768]{0,1:T(8,128)(4,1)S(1)} %iota_compare_fusion, ...), kind=kOutput, calls=%fused_computation.12 | convolution fusion | flops 2491404288 | bytes 62078976 | tf_op jit(solution)/shard_map/transpose(jvp(bkgqs,bskd->bqkgd))/dot_general | solution.py:45
  682.0 26.8 %convert_bitcast_fusion.3 = f32[1,768,8,128]{1,3,2,0:T(8,128)} fusion(bf16[768,8,2,128]{0,3,2,1:T(8,128)(2,1)} %convert_element_type.343, bf16[8,2,768,768]{2,3,1,0:T(8,128)(2,1)} %get-tuple-element.131, f32[8,2,768]{2,1,0:T(2,128)S(1)} %neg.78, f32[8,2,768]{2,1,0:T(2,128)S(1)} %fusion.138, pred[768,768]{0,1:T(8,128)(4,1)S(1)} %iota_compare_fusion, ...), kind=kOutput, calls=%fused_computation.153 | convolution fusion | flops 2502426624 | bytes 63651840 | tf_op jit(solution)/shard_map/transpose(jvp(bqkgd,bskd->bkgqs))/dot_general | solution.py:42
  742.4 26.0 %convert_bitcast_fusion.1 = f32[1,768,8,2,128]{1,4,3,2,0:T(8,128)} fusion(bf16[8,2,768,768]{2,3,1,0:T(8,128)(2,1)} %get-tuple-element.131, f32[8,2,768]{2,1,0:T(2,128)S(1)} %neg.78, f32[8,2,768]{2,1,0:T(2,128)S(1)} %fusion.138, pred[768,768]{0,1:T(8,128)(4,1)S(1)} %iota_compare_fusion, bf16[768,8,128,1]{0,1,2,3:T(8,128)(2,1)S(1)} %bitcast.609, ...), kind=kOutput, calls=%fused_computation.87 | convolution fusion | flops 2503999488 | bytes 65224704 | tf_op jit(solution)/shard_map/transpose(jvp(bqkgd,bskd->bkgqs))/dot_general | solution.py:42
  835.1 18.2 bitcast_convert_fusion.2
  897.3 16.7 fusion.49
  925.0 16.5 multiply_convert_fusion.1
  1087.7 18.1 fusion.21
  1105.8 17.5 fusion.139
  1141.5 23.8 %fusion.17 = (f32[8,2,768]{2,1,0:T(2,128)S(1)}, bf16[8,2,768,768]{2,3,1,0:T(8,128)(2,1)}) fusion(f32[8,2,768]{2,1,0:T(2,128)S(1)} %multiply_divide_fusion, f32[8,2,768]{2,1,0:T(2,128)S(1)} %get-tuple-element.134, f32[8,768,768,2]{2,1,3,0:T(8,128)} %get-tuple-element.135, pred[768,768]{0,1:T(8,128)(4,1)S(1)} %copy-done.1, ...), kind=kOutput, calls=%fused_computation.21 | convolution fusion | flops 2491404288 | bytes 62078976 | tf_op jit(solution)/shard_map/transpose(jvp(bkgqs,bskd->bqkgd))/dot_general | solution.py:45
  1165.4 26.3 %convert_bitcast_fusion.2 = f32[1,768,8,128]{1,3,2,0:T(8,128)} fusion(bf16[768,8,2,128]{0,3,2,1:T(8,128)(2,1)} %convert_element_type.366, bf16[8,2,768,768]{2,3,1,0:T(8,128)(2,1)} %get-tuple-element.137, f32[8,2,768]{2,1,0:T(2,128)S(1)} %neg.84, f32[8,2,768]{2,1,0:T(2,128)S(1)} %fusion.139, pred[768,768]{0,1:T(8,128)(4,1)S(1)} %copy-done.1, ...), kind=kOutput, calls=%fused_computation.152 | convolution fusion | flops 2502426624 | bytes 63651840 | tf_op jit(solution)/shard_map/transpose(jvp(bqkgd,bskd->bkgqs))/dot_general | solution.py:42
  1255.3 18.0 bitcast_convert_fusion
  1313.7 27.6 %convert_bitcast_fusion = f32[1,768,8,2,128]{1,4,3,2,0:T(8,128)} fusion(bf16[8,2,768,768]{2,3,1,0:T(8,128)(2,1)} %get-tuple-element.137, f32[8,2,768]{2,1,0:T(2,128)S(1)} %copy-done.115, f32[8,2,768]{2,1,0:T(2,128)S(1)} %copy-done.105, pred[768,768]{0,1:T(8,128)(4,1)S(1)} %copy-done.1, bf16[768,8,128,1]{0,1,2,3:T(8,128)(2,1)} %bitcast.607, ...), kind=kOutput, calls=%fused_computation.86 | convolution fusion | flops 2503999488 | bytes 65224704 | tf_op jit(solution)/shard_map/transpose(jvp(bqkgd,bskd->bkgqs))/dot_general | solution.py:42
  1399.4 16.5 multiply_reduce_fusion.1
  1438.1 17.5 fusion.52
  1463.4 16.6 multiply_convert_fusion
  1560.1 23.7 %all-reduce.14 = (f32[1024]{0:T(1024)S(1)}, f32[2048]{0:T(1024)S(1)}, f32[1024]{0:T(1024)S(1)}, f32[1024]{0:T(1024)S(1)}, f32[2048]{0:T(1024)S(1)}, /*index=5*/f32[1024]{0:T(1024)S(1)}) all-reduce(f32[1024]{0:T(1024)S(1)} %get-tuple-element.80, f32[2048]{0:T(1024)S(1)} %reshape.1710, ...), channel_id=2, replica_groups=mesh['fsdp'=8] {'fsdp'}, use_global_device_ids=true, to_apply=%region_35.36.clone | all-reduce | flops 8192 | bytes 65536
  1598.4 46.7 %reduce-scatter.17.cloned.1.call-done = f32[128,1024]{1,0:T(8,128)} async-done(((f32[1024,1024]{1,0:T(8,128)}), f32[128,1024]{1,0:T(8,128)}) %reduce-scatter.17.cloned.1.call-update) | async-done | bytes 524304 | tf_op jit(solution)/shard_map/reduce_scatter | solution.py:114
  1645.1 46.6 %reduce-scatter.19.cloned.1.call-done = f32[128,1024]{1,0:T(8,128)} async-done(((f32[1024,1024]{1,0:T(8,128)}), f32[128,1024]{1,0:T(8,128)}) %reduce-scatter.19.cloned.1.call-update) | async-done | bytes 524304 | tf_op jit(solution)/shard_map/reduce_scatter | solution.py:114
  1691.6 87.9 %reduce-scatter.39.cloned.1.call-done = f32[128,3072]{1,0:T(8,128)} async-done(((f32[1024,3072]{1,0:T(8,128)}), f32[128,3072]{1,0:T(8,128)}) %reduce-scatter.39.cloned.1.call-update) | async-done | bytes 1572880 | tf_op jit(solution)/shard_map/reduce_scatter | solution.py:114
  1779.5 88.0 %reduce-scatter.37.cloned.1.call-done = f32[128,3072]{1,0:T(8,128)} async-done(((f32[1024,3072]{1,0:T(8,128)}), f32[128,3072]{1,0:T(8,128)}) %reduce-scatter.37.cloned.1.call-update) | async-done | bytes 1572880 | tf_op jit(solution)/shard_map/reduce_scatter | solution.py:114
  1867.5 87.9 %reduce-scatter.27.cloned.1.call-done = f32[384,1024]{1,0:T(8,128)} async-done(((f32[3072,1024]{1,0:T(8,128)}), f32[384,1024]{1,0:T(8,128)}) %reduce-scatter.27.cloned.1.call-update) | async-done | bytes 1572880 | tf_op jit(solution)/shard_map/reduce_scatter | solution.py:114
  1955.4 67.2 %reduce-scatter.15.cloned.1.call-done = f32[128,2048]{1,0:T(8,128)} async-done(((f32[1024,2048]{1,0:T(8,128)}), f32[128,2048]{1,0:T(8,128)}) %reduce-scatter.15.cloned.1.call-update) | async-done | bytes 1048592 | tf_op jit(solution)/shard_map/reduce_scatter | solution.py:114
  2022.5 88.0 %reduce-scatter.23.cloned.1.call-done = f32[128,3072]{1,0:T(8,128)} async-done(((f32[1024,3072]{1,0:T(8,128)}), f32[128,3072]{1,0:T(8,128)}) %reduce-scatter.23.cloned.1.call-update) | async-done | bytes 1572880 | tf_op jit(solution)/shard_map/reduce_scatter | solution.py:114
  2110.5 88.0 %reduce-scatter.25.cloned.1.call-done = f32[128,3072]{1,0:T(8,128)} async-done(((f32[1024,3072]{1,0:T(8,128)}), f32[128,3072]{1,0:T(8,128)}) %reduce-scatter.25.cloned.1.call-update) | async-done | bytes 1572880 | tf_op jit(solution)/shard_map/reduce_scatter | solution.py:114
  (667 shorter events, 1113.4 us)
Async XLA Ops:
  14.0 435.8 %all-gather.63.cloned.1.call-start = ((), (), s32[]{:S(2)}) async-start(), calls=%async_computation.25 | async-start | bytes 7077888 | tf_op jit(solution)/shard_map/all_gather | solution.py:110
  14.8 445.9 %all-gather.65.cloned.1.call-start = ((), (), s32[]{:S(2)}) async-start(), calls=%async_computation.26 | async-start | bytes 7077888 | tf_op jit(solution)/shard_map/all_gather | solution.py:110
  15.4 458.9 %all-gather.67.cloned.1.call-start = ((), (), s32[]{:S(2)}) async-start(), calls=%async_computation.27 | async-start | bytes 7077888 | tf_op jit(solution)/shard_map/all_gather | solution.py:110
  16.1 502.8 %all-gather.61.cloned.1.call-start = ((), (), s32[]{:S(2)}) async-start(), calls=%async_computation.24 | async-start | bytes 4718592 | tf_op jit(solution)/shard_map/all_gather | solution.py:110
  16.7 628.6 %all-gather.75.cloned.1.call-start = ((), (), s32[]{:S(2)}) async-start(), calls=%async_computation.31 | async-start | bytes 4718592 | tf_op jit(solution)/shard_map/all_gather | solution.py:110
  527.7 386.3 %all-gather.79.cloned.1.call-start = ((), (), s32[]{:S(2)}) async-start(), calls=%async_computation.33 | async-start | bytes 2359296 | tf_op jit(solution)/shard_map/all_gather | solution.py:110
  528.3 391.5 %all-gather.81.cloned.1.call-start = ((), (), s32[]{:S(2)}) async-start(), calls=%async_computation.34 | async-start | bytes 2359296 | tf_op jit(solution)/shard_map/all_gather | solution.py:110
  528.9 396.2 %all-gather.69.cloned.1.call-start = ((), (), s32[]{:S(2)}) async-start(), calls=%async_computation.28 | async-start | bytes 7077888 | tf_op jit(solution)/shard_map/all_gather | solution.py:110
  529.4 412.1 %all-gather.73.cloned.1.call-start = ((), (), s32[]{:S(2)}) async-start(), calls=%async_computation.30 | async-start | bytes 7077888 | tf_op jit(solution)/shard_map/all_gather | solution.py:110
  530.2 421.1 %all-gather.71.cloned.1.call-start = ((), (), s32[]{:S(2)}) async-start(), calls=%async_computation.29 | async-start | bytes 7077888 | tf_op jit(solution)/shard_map/all_gather | solution.py:110
  530.8 430.5 %all-gather.77.cloned.1.call-start = ((), (), s32[]{:S(2)}) async-start(), calls=%async_computation.32 | async-start | bytes 4718592 | tf_op jit(solution)/shard_map/all_gather | solution.py:110
  645.2 483.8 %all-gather.89.cloned.1.call-start = ((), (), s32[]{:S(2)}) async-start(), calls=%async_computation.38 | async-start | bytes 4718592 | tf_op jit(solution)/shard_map/all_gather | solution.py:110
  977.3 486.1 %all-gather.83.cloned.1.call-start = ((), (), s32[]{:S(2)}) async-start(), calls=%async_computation.35 | async-start | bytes 7077888 | tf_op jit(solution)/shard_map/all_gather | solution.py:110
  978.0 535.3 %all-gather.93.cloned.1.call-start = ((), (), s32[]{:S(2)}) async-start(), calls=%async_computation.40 | async-start | bytes 2359296 | tf_op jit(solution)/shard_map/all_gather | solution.py:110
  978.6 540.3 %all-gather.95.cloned.1.call-start = ((), (), s32[]{:S(2)}) async-start(), calls=%async_computation.41 | async-start | bytes 2359296 | tf_op jit(solution)/shard_map/all_gather | solution.py:110
  979.3 545.2 %all-gather.87.cloned.1.call-start = ((), (), s32[]{:S(2)}) async-start(), calls=%async_computation.37 | async-start | bytes 7077888 | tf_op jit(solution)/shard_map/all_gather | solution.py:110
  979.9 554.6 %all-gather.85.cloned.1.call-start = ((), (), s32[]{:S(2)}) async-start(), calls=%async_computation.36 | async-start | bytes 7077888 | tf_op jit(solution)/shard_map/all_gather | solution.py:110
  980.5 564.4 %all-gather.91.cloned.1.call-start = ((), (), s32[]{:S(2)}) async-start(), calls=%async_computation.39 | async-start | bytes 4718592 | tf_op jit(solution)/shard_map/all_gather | solution.py:110
  981.2 610.2 %reduce-scatter.35.cloned.1.call-start = ((), (), s32[]{:S(2)}) async-start(), calls=%async_computation.52 | async-start | bytes 9437184 | tf_op jit(solution)/shard_map/reduce_scatter | solution.py:114
  989.0 602.4 %reduce-scatter.31.cloned.1.call-start = ((), (), s32[]{:S(2)}) async-start(), calls=%async_computation.50 | async-start | bytes 4718592 | tf_op jit(solution)/shard_map/reduce_scatter | solution.py:114
  995.2 596.2 %reduce-scatter.33.cloned.1.call-start = ((), (), s32[]{:S(2)}) async-start(), calls=%async_computation.51 | async-start | bytes 4718592 | tf_op jit(solution)/shard_map/reduce_scatter | solution.py:114
  1000.9 590.6 %reduce-scatter.41.cloned.1.call-start = ((), (), s32[]{:S(2)}) async-start(), calls=%async_computation.55 | async-start | bytes 14155776 | tf_op jit(solution)/shard_map/reduce_scatter | solution.py:114
  1011.4 580.0 %reduce-scatter.29.cloned.1.call-start = ((), (), s32[]{:S(2)}) async-start(), calls=%async_computation.49 | async-start | bytes 9437184 | tf_op jit(solution)/shard_map/reduce_scatter | solution.py:114
  1019.4 578.9 %reduce-scatter.21.cloned.1.call-start = ((), (), s32[]{:S(2)}) async-start(), calls=%async_computation.45 | async-start | bytes 9437184 | tf_op jit(solution)/shard_map/reduce_scatter | solution.py:114
  1129.0 516.1 %reduce-scatter.17.cloned.1.call-start = ((), (), s32[]{:S(2)}) async-start(), calls=%async_computation.43 | async-start | bytes 4718592 | tf_op jit(solution)/shard_map/reduce_scatter | solution.py:114
  1255.3 436.4 %reduce-scatter.19.cloned.1.call-start = ((), (), s32[]{:S(2)}) async-start(), calls=%async_computation.44 | async-start | bytes 4718592 | tf_op jit(solution)/shard_map/reduce_scatter | solution.py:114
  1278.7 500.8 %reduce-scatter.39.cloned.1.call-start = ((), (), s32[]{:S(2)}) async-start(), calls=%async_computation.54 | async-start | bytes 14155776 | tf_op jit(solution)/shard_map/reduce_scatter | solution.py:114
  1290.7 576.8 %reduce-scatter.37.cloned.1.call-start = ((), (), s32[]{:S(2)}) async-start(), calls=%async_computation.53 | async-start | bytes 14155776 | tf_op jit(solution)/shard_map/reduce_scatter | solution.py:114
  1302.1 653.2 %reduce-scatter.27.cloned.1.call-start = ((), (), s32[]{:S(2)}) async-start(), calls=%async_computation.48 | async-start | bytes 14155776 | tf_op jit(solution)/shard_map/reduce_scatter | solution.py:114
  1312.5 710.0 %reduce-scatter.15.cloned.1.call-start = ((), (), s32[]{:S(2)}) async-start(), calls=%async_computation.42 | async-start | bytes 9437184 | tf_op jit(solution)/shard_map/reduce_scatter | solution.py:114
  1463.3 647.2 %reduce-scatter.23.cloned.1.call-start = ((), (), s32[]{:S(2)}) async-start(), calls=%async_computation.46 | async-start | bytes 14155776 | tf_op jit(solution)/shard_map/reduce_scatter | solution.py:114
  1490.9 707.6 %reduce-scatter.25.cloned.1.call-start = ((), (), s32[]{:S(2)}) async-start(), calls=%async_computation.47 | async-start | bytes 14155776 | tf_op jit(solution)/shard_map/reduce_scatter | solution.py:114
  (157 other events, 7484.6 us)
Sparse Core Ops, SparseCore 0:
  60.8 31.0 all-gather.44
  93.5 39.8 all-gather.48
  135.0 39.8 all-gather.50
  176.6 39.8 all-gather.52
  218.2 31.0 all-gather.46
  299.1 31.0 all-gather.58
  332.0 39.8 all-gather.62
  373.5 39.8 all-gather.64
  415.2 39.8 all-gather.66
  456.7 31.0 all-gather.60
  608.2 39.8 all-gather.68
  649.9 39.8 all-gather.72
  691.4 39.8 all-gather.70
  977.4 31.8 all-gather.88
  1011.1 39.8 all-gather.82
  1100.6 39.8 all-gather.86
  1142.1 39.8 all-gather.84
  1183.8 31.0 all-gather.90
  1218.8 63.1 reduce-scatter.34
  1285.7 42.8 reduce-scatter.30
  1332.4 42.8 reduce-scatter.32
  1379.3 83.9 reduce-scatter.40
  1467.1 63.1 reduce-scatter.28
  1534.3 64.0 reduce-scatter.20
  1602.2 42.8 reduce-scatter.16
  1648.8 42.8 reduce-scatter.18
  1695.5 83.9 reduce-scatter.38
  1783.5 83.9 reduce-scatter.36
  1871.4 83.9 reduce-scatter.26
  1959.3 63.1 reduce-scatter.14
  2026.5 83.9 reduce-scatter.22
  2114.6 83.9 reduce-scatter.24
  (10 shorter events, 241.8 us)
where the time goes:
time: 2220 us; the launch traced here: 2210 us
  matrix products  663 us (30%)
  waiting for transfers between devices  623 us (28%)
  other arithmetic  426 us (19%)
  local copies, waits for them, and re-layouts  335 us (15%)
  blocking collectives  141 us (6%)
    reduce_scatter x14, waiting for transfers between devices, reduce_shards(): lax.psum_scatter(part_grad, FSDP_AXIS, scatter_dimension=0, tiled=True)  607 us
    dot_general x8, matrix products, attention_core(): jnp.einsum('bqkgd,bskd->bkgqs', q_grp, k_rot, preferred_element_type=jnp....  179 us
    dot_general x6, matrix products, attention_core(): jnp.einsum('bkgqs,bskd->bqkgd', attn_prob, v_heads, preferred_element_typ...  122 us
    all_gather x12, blocking collectives, gather_full(): lax.all_gather(param_piece, FSDP_AXIS, axis=0, tiled=True)  117 us
    reduce_sum x4, other arithmetic, attention_core(): jax.nn.softmax(jnp.where(causal, scores, -1e+30), axis=-1)  66.5 us
    reduce_sum x10, other arithmetic, layer_norm32(): return centered * lax.rsqrt(variance + EPSILON) * weight  66.4 us
    unnamed x306, local copies, waits for them, and re-layouts  51 us
    another operation x8, other arithmetic  50 us
  transfers between devices with their start and end apart: 42, of which 9 were waited for; matrix products, arithmetic and copies ran while one was open for 62% of the time, Pallas kernels for 0%

commit v1 on v0

v1 whole, which is shorter than its diff:
```python
import jax
import jax.numpy as jnp
from jax import lax
from jax.experimental import pallas as pl
from jax.experimental.pallas import tpu as pltpu
from jax.sharding import PartitionSpec as P


HEAD_DIM = 128
EPSILON = 1e-5
ROPE_THETA = 7.5e7
AXIS = 'fsdp'
F32 = jnp.float32
BF16 = jnp.bfloat16
VMEM_LIMIT = 60 * 1024 * 1024
CORE_BIT, X_BIT, Y_BIT = 1, 2, 4
ORDER_X_FIRST = (3, 7, 1, 5, 2, 6, 0, 4)
ORDER_Y_FIRST = (5, 7, 1, 3, 4, 6, 0, 2)


def dot_nn(a, b):
    return lax.dot_general(a, b, (((1,), (0,)), ((), ())), preferred_element_type=F32)


def dot_nt(a, b):
    return lax.dot_general(a, b, (((1,), (1,)), ((), ())), preferred_element_type=F32)


def dot_tn(a, b):
    return lax.dot_general(a, b, (((0,), (0,)), ((), ())), preferred_element_type=F32)


def call(kernel, grid, in_specs, out_specs, out_shape, flops, nbytes, scratch=(), prefetch=0, trans=0):
    return pl.pallas_call(
        kernel,
        grid_spec=pltpu.PrefetchScalarGridSpec(
            num_scalar_prefetch=prefetch, grid=grid, in_specs=in_specs, out_specs=out_specs, scratch_shapes=list(scratch)),
        out_shape=out_shape,
        cost_estimate=pl.CostEstimate(flops=flops, bytes_accessed=nbytes, transcendentals=trans),
        compiler_params=pltpu.CompilerParams(vmem_limit_bytes=VMEM_LIMIT))


def sds(shape, dtype):
    return jax.ShapeDtypeStruct(shape, dtype)


def norm_blocks(stream, gain, order_x, order_y):
    tokens, width = stream.shape
    block = width // 8

    def kernel(ox_ref, oy_ref, x_ref, g_ref, n_ref, nx_ref, ny_ref):
        hat, _ = width_norm(x_ref[...])
        n_ref[...] = (hat * g_ref[...]).astype(BF16)
        for j in range(8):
            cols = slice(j * block, (j + 1) * block)
            nx_ref[:, cols] = n_ref[:, pl.ds(pl.multiple_of(ox_ref[j] * block, block), block)]
            ny_ref[:, cols] = n_ref[:, pl.ds(pl.multiple_of(oy_ref[j] * block, block), block)]

    whole = pl.BlockSpec((tokens, width), lambda i, ox, oy: (0, 0))
    return call(kernel, (1,), [whole, pl.BlockSpec((1, width), lambda i, ox, oy: (0, 0))], [whole] * 3,
                [sds((tokens, width), BF16)] * 3, 10 * tokens * width, 8 * tokens * width,
                prefetch=2)(order_x, order_y, stream, gain[None])


def project(values, weights, column, width, tile=512):
    tokens, depth = values.shape
    first = column // tile

    def kernel(x_ref, w_ref, o_ref):
        o_ref[...] = dot_nn(x_ref[...], w_ref[...])

    return call(kernel, (width // tile,),
                [pl.BlockSpec((tokens, depth), lambda j: (0, 0)),
                 pl.BlockSpec((depth, tile), lambda j: (0, first + j))],
                pl.BlockSpec((tokens, tile), lambda j: (0, j)),
                sds((tokens, width), F32), 2 * tokens * depth * width,
                2 * depth * width + 4 * tokens * width)(values, weights)


def swiglu_forward(values, weights, column, width, place_x, place_y):
    tokens, depth = values.shape
    tile = width // 8
    first = column // tile

    def kernel(px_ref, py_ref, x_ref, wg_ref, wu_ref, g_ref, u_ref, m_ref, mx_ref, my_ref):
        x = x_ref[...]
        gate = dot_nn(x, wg_ref[...])
        up = dot_nn(x, wu_ref[...])
        g_ref[...] = gate
        u_ref[...] = up
        hidden = (gate * jax.nn.sigmoid(gate) * up).astype(BF16)
        m_ref[...] = hidden
        mx_ref[...] = hidden
        my_ref[...] = hidden

    col = pl.BlockSpec((tokens, tile), lambda j, px, py: (0, j))
    return call(kernel, (8,),
                [pl.BlockSpec((tokens, depth), lambda j, px, py: (0, 0)),
                 pl.BlockSpec((depth, tile), lambda j, px, py: (0, first + j)),
                 pl.BlockSpec((depth, tile), lambda j, px, py: (0, first + 8 + j))],
                [col, col, col, pl.BlockSpec((tokens, tile), lambda j, px, py: (0, px[j])),
                 pl.BlockSpec((tokens, tile), lambda j, px, py: (0, py[j]))],
                [sds((tokens, width), F32)] * 2 + [sds((tokens, width), BF16)] * 3,
                4 * tokens * depth * width, 4 * depth * width + 14 * tokens * width,
                trans=tokens * width, prefetch=2)(place_x, place_y, values, weights, weights)


def output_projection(stream, attn, hidden, weights, tile=256):
    tokens, model = stream.shape
    parts, rows, _ = weights.shape
    attn_w, hid_w = attn.shape[1], hidden.shape[1]
    attn_rows = attn_w // parts

    def kernel(x_ref, a_ref, m_ref, w_ref, y_ref):
        w_o = w_ref[:, :attn_rows, :].reshape(attn_w, tile)
        w_d = w_ref[:, attn_rows:, :].reshape(hid_w, tile)
        total = x_ref[...].astype(F32) + dot_nn(a_ref[...], w_o) + dot_nn(m_ref[...], w_d)
        y_ref[...] = total.astype(BF16)

    col = pl.BlockSpec((tokens, tile), lambda j: (0, j))
    return call(kernel, (model // tile,),
                [col, pl.BlockSpec((tokens, attn_w), lambda j: (0, 0)),
                 pl.BlockSpec((tokens, hid_w), lambda j: (0, 0)),
                 pl.BlockSpec((parts, rows, tile), lambda j: (0, 0, j))],
                col, sds((tokens, model), BF16), 2 * tokens * model * (attn_w + hid_w),
                2 * (attn_w + hid_w) * (model + tokens))(stream, attn, hidden, weights)


def output_backward(grad_y, weights, gate, up, attn_w):
    tokens, model = grad_y.shape
    parts, rows, _ = weights.shape
    hid_w = gate.shape[1]
    ar, hr = attn_w // parts, hid_w // parts

    def kernel(gy_ref, w_ref, g_ref, u_ref, da_ref, dg_ref, du_ref):
        gy = gy_ref[...]
        da_ref[...] = dot_nt(gy, w_ref[0, :ar, :]).astype(BF16)
        d_hidden = dot_nt(gy, w_ref[0, ar:, :])
        gate_v = g_ref[...]
        sig = jax.nn.sigmoid(gate_v)
        silu = gate_v * sig
        du_ref[...] = (d_hidden * silu).astype(BF16)
        dg_ref[...] = (d_hidden * u_ref[...] * (sig + silu * (1.0 - sig))).astype(BF16)

    def col(width):
        return pl.BlockSpec((tokens, width), lambda j: (0, j))

    return call(kernel, (parts,),
                [pl.BlockSpec((tokens, model), lambda j: (0, 0)),
                 pl.BlockSpec((1, rows, model), lambda j: (j, 0, 0)), col(hr), col(hr)],
                [col(ar), col(hr), col(hr)],
                [sds((tokens, attn_w), BF16), sds((tokens, hid_w), BF16), sds((tokens, hid_w), BF16)],
                2 * tokens * model * (attn_w + hid_w),
                2 * (attn_w + hid_w) * model + 12 * tokens * hid_w + 2 * tokens * attn_w,
                trans=tokens * hid_w)(grad_y, weights, gate, up)


def input_backward(pieces, tile=512):
    tokens = pieces[0][0].shape[0]
    depth = pieces[0][1].shape[0]
    total = None
    for grads, weights, column in pieces:
        steps = grads.shape[1] // tile
        first = column // tile
        has_total = total is not None

        def kernel(*refs, steps=steps, has_total=has_total):
            d_ref, w_ref = refs[0], refs[1]
            o_ref = refs[-1]
            part = dot_nt(d_ref[...], w_ref[...])

            @pl.when(pl.program_id(0) == 0)
            def _():
                o_ref[...] = part + refs[2][...] if has_total else part

            @pl.when(pl.program_id(0) > 0)
            def _():
                o_ref[...] += part

        whole = pl.BlockSpec((tokens, depth), lambda j: (0, 0))
        specs = [pl.BlockSpec((tokens, tile), lambda j: (0, j)),
                 pl.BlockSpec((depth, tile), lambda j, first=first: (0, first + j))]
        args = [grads, weights]
        if has_total:
            specs.append(whole)
            args.append(total)
        total = call(kernel, (steps,), specs, whole, sds((tokens, depth), F32),
                     2 * tokens * depth * tile * steps, 2 * (tokens + depth) * tile * steps + 4 * tokens * depth)(*args)
    return total


def swap_pairs(values):
    lane = lax.broadcasted_iota(jnp.int32, values.shape, 1)
    return jnp.where(lane % 2 == 0, pltpu.roll(values, HEAD_DIM - 1, 1), pltpu.roll(values, 1, 1))


def head_norm(values):
    mean = jnp.mean(values, axis=-1, keepdims=True)
    centered = values - mean
    rstd = lax.rsqrt(jnp.mean(centered * centered, axis=-1, keepdims=True) + EPSILON)
    return centered * rstd, rstd


def rope(values, cos, sin):
    return values * cos + swap_pairs(values) * sin


def scores_t(k, q, start):
    keys = lax.broadcasted_iota(jnp.int32, (k.shape[0], q.shape[0]), 0)
    queries = lax.broadcasted_iota(jnp.int32, (k.shape[0], q.shape[0]), 1) + start
    s = jnp.where(queries >= keys, dot_nt(k, q) * HEAD_DIM ** -0.5, -1e30)
    e = jnp.exp(s - jnp.max(s, axis=0, keepdims=True))
    return e * (1.0 / jnp.sum(e, axis=0, keepdims=True))


def attention_specs(tokens):
    table = pl.BlockSpec((tokens, HEAD_DIM), lambda h, *_: (0, 0))
    return [pl.BlockSpec((tokens, 512), lambda h, *_: (0, h)),
            pl.BlockSpec((1, 2, HEAD_DIM), lambda h, *_: (h, 0, 0)),
            pl.BlockSpec((1, 1, HEAD_DIM), lambda h, *_: (h, 0, 0)), table, table]


def attention_forward(qkv, q_norm, k_norm, cos, sin, place, block=256):
    tokens = qkv.shape[0]
    groups = qkv.shape[1] // 512

    def kernel(place_ref, qkv_ref, qn_ref, kn_ref, cos_ref, sin_ref, o_ref, op_ref):
        cos_v, sin_v = cos_ref[...], sin_ref[...]
        k = rope(head_norm(qkv_ref[:, 256:384])[0] * kn_ref[0], cos_v, sin_v).astype(BF16)
        v_t = qkv_ref[:, 384:512].T.astype(BF16)
        for head in range(2):
            cols = slice(head * HEAD_DIM, (head + 1) * HEAD_DIM)
            q = rope(head_norm(qkv_ref[:, cols])[0] * qn_ref[0, head:head + 1, :], cos_v, sin_v).astype(BF16)
            for start in range(0, tokens, block):
                stop = start + block
                prob = scores_t(k[:stop], q[start:stop], start).astype(BF16)
                out = dot_nn(v_t[:, :stop], prob).T.astype(BF16)
                o_ref[start:stop, cols] = out
                op_ref[start:stop, cols] = out

    return call(kernel, (groups,), attention_specs(tokens),
                [pl.BlockSpec((tokens, 256), lambda h, p: (0, h)), pl.BlockSpec((tokens, 256), lambda h, p: (0, p[h]))],
                [sds((tokens, groups * 256), BF16)] * 2,
                groups * 2 * 4 * tokens * tokens * HEAD_DIM, 4 * tokens * groups * 512 + 4 * tokens * groups * 256,
                trans=groups * 2 * tokens * tokens, prefetch=1)(place, qkv, q_norm, k_norm, cos, sin)


def attention_backward(qkv, d_attn, q_norm, k_norm, cos, sin, block=256):
    tokens = qkv.shape[0]
    groups = qkv.shape[1] // 512

    def norm_back(d_rot, hat, rstd, gain, cos_v, sin_v):
        d_rot = d_rot.astype(BF16).astype(F32)
        d_out = d_rot * cos_v - swap_pairs(d_rot) * sin_v
        d_gain = jnp.sum(d_out * hat, axis=0, keepdims=True)
        d_hat = d_out * gain
        d_in = rstd * (d_hat - jnp.mean(d_hat, axis=-1, keepdims=True)
                       - hat * jnp.mean(d_hat * hat, axis=-1, keepdims=True))
        return d_in.astype(BF16), d_gain

    def kernel(qkv_ref, qn_ref, kn_ref, cos_ref, sin_ref, do_ref, d_ref, gq_ref, gk_ref, dk_acc, dv_acc, dq_acc):
        cos_v, sin_v = cos_ref[...], sin_ref[...]
        k_hat, k_rstd = head_norm(qkv_ref[:, 256:384])
        k_rot = rope(k_hat * kn_ref[0], cos_v, sin_v)
        k = k_rot.astype(BF16)
        k_t = k_rot.T.astype(BF16)
        v = qkv_ref[:, 384:512].astype(BF16)
        dk_acc[...] = jnp.zeros_like(dk_acc)
        dv_acc[...] = jnp.zeros_like(dv_acc)
        for head in range(2):
            cols = slice(head * HEAD_DIM, (head + 1) * HEAD_DIM)
            q_hat, q_rstd = head_norm(qkv_ref[:, cols])
            q = rope(q_hat * qn_ref[0, head:head + 1, :], cos_v, sin_v).astype(BF16)
            for start in range(0, tokens, block):
                stop = start + block
                q_b = q[start:stop]
                do_b = do_ref[start:stop, cols]
                prob = scores_t(k[:stop], q_b, start)
                dv_acc[:stop] += dot_nn(prob.astype(BF16), do_b)
                d_prob = dot_nt(v[:stop], do_b).astype(BF16).astype(F32)
                weighted = prob * d_prob
                d_s = weighted - prob * jnp.sum(weighted, axis=0, keepdims=True)
                d_s = (d_s * HEAD_DIM ** -0.5).astype(BF16)
                dk_acc[:stop] += dot_nn(d_s, q_b)
                dq_acc[start:stop, :] = dot_nn(k_t[:, :stop], d_s).T
            d_in, d_gain = norm_back(dq_acc[...], q_hat, q_rstd, qn_ref[0, head:head + 1, :], cos_v, sin_v)
            d_ref[:, cols] = d_in
            gq_ref[0, head:head + 1, :] = d_gain
        d_in, d_gain = norm_back(dk_acc[...], k_hat, k_rstd, kn_ref[0], cos_v, sin_v)
        d_ref[:, 256:384] = d_in
        gk_ref[0] = d_gain
        d_ref[:, 384:512] = dv_acc[...].astype(BF16)

    return call(kernel, (groups,),
                attention_specs(tokens) + [pl.BlockSpec((tokens, 256), lambda h: (0, h))],
                [pl.BlockSpec((tokens, 512), lambda h: (0, h)),
                 pl.BlockSpec((1, 2, HEAD_DIM), lambda h: (h, 0, 0)),
                 pl.BlockSpec((1, 1, HEAD_DIM), lambda h: (h, 0, 0))],
                [sds((tokens, groups * 512), BF16), sds((groups, 2, HEAD_DIM), F32), sds((groups, 1, HEAD_DIM), F32)],
                groups * 2 * 10 * tokens * tokens * HEAD_DIM, 6 * tokens * groups * 512 + 2 * tokens * groups * 256,
                scratch=[pltpu.VMEM((tokens, HEAD_DIM), F32)] * 3,
                trans=groups * 2 * tokens * tokens)(qkv, q_norm, k_norm, cos, sin, d_attn)


def width_norm(stream):
    values = stream.astype(F32)
    centered = values - jnp.mean(values, axis=-1, keepdims=True)
    rstd = lax.rsqrt(jnp.mean(centered * centered, axis=-1, keepdims=True) + EPSILON)
    return centered * rstd, rstd


def width_norm_backward(stream, gain, d_normed):
    hat, rstd = width_norm(stream)
    d_gain = jnp.sum(d_normed * hat, axis=0)
    d_hat = d_normed * gain
    d_in = rstd * (d_hat - jnp.mean(d_hat, axis=-1, keepdims=True)
                   - hat * jnp.mean(d_hat * hat, axis=-1, keepdims=True))
    return d_in, d_gain


def exchange(values, bit):
    return lax.ppermute(values, AXIS, [(i, i ^ bit) for i in range(8)])


def reduce_product(acts, cotangent, x_first):
    rows = acts.shape[1] // 8
    first, second = (X_BIT, Y_BIT) if x_first else (Y_BIT, X_BIT)
    odd = dot_tn(acts[:, :4 * rows], cotangent)
    from_core = exchange(odd, CORE_BIT)
    sent = dot_tn(acts[:, 4 * rows:6 * rows], cotangent) + from_core[:2 * rows]
    from_first = exchange(sent, first)
    kept = dot_tn(acts[:, 6 * rows:], cotangent) + from_core[2 * rows:]
    passed = kept[rows:] + from_first[rows:]
    from_second = exchange(passed, second)
    return kept[:rows] + from_first[:rows] + from_second


def reduce_vector(values):
    me = lax.axis_index(AXIS)
    blocks = values[jnp.array(ORDER_X_FIRST) ^ me]
    from_core = exchange(blocks[:4], CORE_BIT)
    kept = blocks[4:] + from_core
    from_x = exchange(kept[:2], X_BIT)
    kept = kept[2:] + from_x
    return kept[0] + exchange(kept[1], Y_BIT)


def gather(shard):
    return lax.all_gather(shard, AXIS, axis=0, tiled=True)


def solution(mesh):
    act_spec = P(AXIS, None, None)
    vec, mat = P(AXIS), P(AXIS, None)
    param_spec = (vec,) + (mat,) * 7 + (vec, vec)
    in_specs = (act_spec, P(), act_spec) + param_spec + param_spec
    out_specs = (act_spec, act_spec) + param_spec + param_spec

    def body(x_in, positions, grad_out, *shards):
        me = lax.axis_index(AXIS)
        lanes = jnp.arange(8, dtype=jnp.int32)
        order_x = jnp.array(ORDER_X_FIRST, jnp.int32) ^ me
        order_y = jnp.array(ORDER_Y_FIRST, jnp.int32) ^ me
        place_x = jnp.array([ORDER_X_FIRST.index(i) for i in range(8)], jnp.int32)[lanes ^ me]
        place_y = jnp.array([ORDER_Y_FIRST.index(i) for i in range(8)], jnp.int32)[lanes ^ me]
        layers = (shards[:10], shards[10:])

        def in_shard(p):
            rows = p[1].shape[0]
            parts = [p[1].reshape(rows, 8, 256), p[2].reshape(rows, 8, 128), p[3].reshape(rows, 8, 128)]
            qkv = jnp.concatenate(parts, axis=2).reshape(rows, 4096)
            return jnp.concatenate([p[5], p[6], qkv], axis=1)

        def out_shard(p):
            return jnp.concatenate([p[4], p[7]], axis=0)[None]

        one, two = layers
        vectors = gather(jnp.concatenate([one[0], one[8], one[9], two[0], two[8], two[9]])[None])
        w_in, w_out = [], []
        for p in layers:
            w_in.append(gather(in_shard(p)))
            w_out.append(gather(out_shard(p)))
        gains = []
        for base in (0, 512):
            gains.append((vectors[:, base:base + 128].reshape(-1),
                          vectors[:, base + 128:base + 384].reshape(8, 2, 128),
                          vectors[:, base + 384:base + 512].reshape(8, 1, 128)))

        inv_freq = ROPE_THETA ** (-jnp.arange(0, HEAD_DIM, 2, dtype=F32) / HEAD_DIM)
        angles = positions.astype(F32)[:, None] * jnp.repeat(inv_freq, 2)[None, :]
        cos = jnp.cos(angles)
        sin = jnp.sin(angles) * jnp.where(jnp.arange(HEAD_DIM) % 2 == 0, -1.0, 1.0)[None, :]

        stream = x_in[0]
        saved = []
        for index in range(2):
            ln_gain, q_gain, k_gain = gains[index]
            normed, normed_x, normed_y = norm_blocks(stream, ln_gain, order_x, order_y)
            qkv = project(normed, w_in[index], 6144, 4096)
            gate, up, *hidden = swiglu_forward(normed, w_in[index], 0, 3072, place_x, place_y)
            attn = attention_forward(qkv, q_gain, k_gain, cos, sin, place_x if index else place_y)
            saved.append((stream, normed_x, normed_y, qkv, attn[1], gate, up, hidden))
            stream = output_projection(stream, attn[0], hidden[0], w_out[index])
        y_out = stream

        grad = grad_out[0]
        results = [None, None]
        for index in (1, 0):
            ln_gain, q_gain, k_gain = gains[index]
            stream, normed_x, normed_y, qkv, attn, gate, up, hidden = saved[index]
            g_down = jnp.concatenate([reduce_product(hidden[1], grad[:, :512], True),
                                      reduce_product(hidden[2], grad[:, 512:], False)], axis=1)
            d_attn, d_gate, d_up = output_backward(grad, w_out[index], gate, up, attn.shape[1])
            g_gate = reduce_product(normed_x, d_gate, True)
            g_up = reduce_product(normed_y, d_up, False)
            g_o = reduce_product(attn, grad, index == 1)
            d_qkv, g_qn, g_kn = attention_backward(qkv, d_attn, q_gain, k_gain, cos, sin)
            g_qkv = jnp.concatenate([reduce_product(normed_x, d_qkv[:, :2048], True),
                                     reduce_product(normed_y, d_qkv[:, 2048:], False)], axis=1)
            d_normed = input_backward([(d_gate, w_in[index], 0), (d_up, w_in[index], 3072),
                                       (d_qkv, w_in[index], 6144)])
            d_stream, g_ln = width_norm_backward(stream, ln_gain, d_normed)
            grad = (grad.astype(F32) + d_stream).astype(BF16)
            g_vec = reduce_vector(jnp.concatenate(
                [g_ln.reshape(8, 128), g_qn.reshape(8, 256), g_kn.reshape(8, 128)], axis=1))
            split = g_qkv.reshape(128, 8, 512)
            results[index] = (g_vec[:128], split[:, :, :256].reshape(128, 2048), split[:, :, 256:384].reshape(128, 1024),
                              split[:, :, 384:].reshape(128, 1024), g_o, g_gate, g_up, g_down,
                              g_vec[128:384], g_vec[384:])
        return (y_out[None], grad[None]) + results[0] + results[1]

    return jax.shard_map(body, mesh=mesh, in_specs=in_specs, out_specs=out_specs, check_vma=False)
```

time: 2220 us -> 1330 us (0.60)
  matrix products: 663 us -> 164 us
  Pallas kernels: 0 us -> 406 us
  other arithmetic: 426 us -> 60.2 us
  local copies, waits for them, and re-layouts: 335 us -> 35.8 us
  blocking collectives: 141 us -> 13.1 us
  starting transfers between devices: 1.66 us -> 33.8 us
  waiting for transfers between devices: 623 us -> 591 us
    reduce_scatter x14 -> x0, waiting for transfers between devices: 607 us -> none  [reduce_shards(): lax.psum_scatter(part_grad, FSDP_AXIS, scatter_dimension=0, tiled=True)]
    dot_general x56 -> x42, matrix products: 663 us -> 164 us  [dot_tn(): lax.dot_general(a, b, (((0,), (0,)), ((), ())), preferred_element_type=F32)]
    ppermute x0 -> x48, waiting for transfers between devices: none -> 449 us  [exchange(): return lax.ppermute(values, AXIS, [(i, i ^ bit) for i in range(8)])]
    pallas_call x0 -> x20, Pallas kernels: none -> 406 us  [the longest x2 109 us: attention_backward(): call(kernel, (groups,), attention_specs(tokens) + [pl.BlockSpec((tokens,...]
    reduce_sum x25 -> x6, other arithmetic: 162 us -> 8.09 us  [the longest x2 6.43 us: width_norm_backward(): d_gain = jnp.sum(d_normed * hat, axis=0)]
    all_gather x28 -> x4, waiting for transfers between devices: 0.19 us -> 142 us  [gather(): return lax.all_gather(shard, AXIS, axis=0, tiled=True)]
    reshape x24 -> x4, local copies, waits for them, and re-layouts: 119 us -> 2.37 us  [the longest x3 1.21 us: body(): vectors[:, base + 128:base + 384].reshape(8, 2, 128)]
    all_gather x12 -> x1, blocking collectives: 117 us -> 13.1 us  [gather(): return lax.all_gather(shard, AXIS, axis=0, tiled=True)]
  transfers between devices with their start and end apart: 42 -> 52, of which waited for: 9 -> 24; matrix products, arithmetic and copies ran while one was open for 62% -> 19% of each run, Pallas kernels for 0% -> 31%
where the time goes in v1:
time: 1330 us; the launch traced here: 1320 us
  waiting for transfers between devices  591 us (44%)
  Pallas kernels  406 us (31%)
  matrix products  164 us (12%)
  other arithmetic  60.2 us (5%)
  local copies, waits for them, and re-layouts  35.8 us (3%)
  starting transfers between devices  33.8 us (3%)
  between operations  15.5 us (1%)
    ppermute x48, waiting for transfers between devices, exchange(): return lax.ppermute(values, AXIS, [(i, i ^ bit) for i in range(8)])  449 us
    dot_general x42, matrix products, dot_tn(): lax.dot_general(a, b, (((0,), (0,)), ((), ())), preferred_element_type=F32)  164 us
    all_gather x4, waiting for transfers between devices, gather(): return lax.all_gather(shard, AXIS, axis=0, tiled=True)  142 us
    pallas_call x2, Pallas kernels, attention_backward(): call(kernel, (groups,), attention_specs(tokens) + [pl.BlockSpec((tokens,...  109 us
    pallas_call x6, Pallas kernels, input_backward(): call(kernel, (steps,), specs, whole, sds((tokens, depth), F32), 2 * token...  78.1 us
    pallas_call x2, Pallas kernels, attention_forward(): call(kernel, (groups,), attention_specs(tokens), [pl.BlockSpec((tokens, 2...  68.9 us
    pallas_call x2, Pallas kernels, swiglu_forward(): call(kernel, (8,), [pl.BlockSpec((tokens, depth), lambda j, px, py: (0, 0...  43.4 us
    pallas_call x2, Pallas kernels, output_backward(): call(kernel, (parts,), [pl.BlockSpec((tokens, model), lambda j: (0, 0)),...  40.6 us
  transfers between devices with their start and end apart: 52, of which 24 were waited for; matrix products, arithmetic and copies ran while one was open for 19% of the time, Pallas kernels for 31%

profile of v1, /device:TPU:0, one launch (start us, length us, event | category | flops | bytes accessed | tf_op | source)
XLA Modules:
  0.0 1319.7 jit_solution(13325363034935494635)
XLA Ops:
  21.4 13.1 all-gather
  49.7 68.2 %all-gather.8.cloned.1.call-done.w_ref.wg_ref.wu_ref.refs_1_ = bf16[1024,10240]{1,0:T(8,128)(2,1)} async-done(((bf16[128,10240]{1,0:T(8,128)(2,1)}), bf16[1024,10240]{1,0:T(8,128)(2,1)}) %all-gather.8.cloned.1.call-update) | async-done | bytes 20971536 | tf_op jit(solution)/shard_map/all_gather | solution.py:349
  117.8 13.6 %shard_map.445.qkv_ref = f32[768,4096]{1,0:T(8,128)} custom-call(bf16[768,1024]{1,0:T(8,128)(2,1)} %get-tuple-element.54.x_ref, bf16[1024,10240]{1,0:T(8,128)(2,1)} %all-gather.8.cloned.1.call-done.w_ref.wg_ref.wu_ref.refs_1_), custom_call_target="tpu_custom_call" | custom-call | flops 6442450944 | bytes 20971520 | tf_op jit(solution)/shard_map/pallas_call | solution.py:72
  131.4 34.4 %shard_map.446 = (bf16[768,2048]{1,0:T(8,128)(2,1)}, bf16[768,2048]{1,0:T(8,128)(2,1)}) custom-call(s32[8]{0:T(128)} %gather_fusion, f32[768,4096]{1,0:T(8,128)} %shard_map.445.qkv_ref, f32[8,2,128]{2,1,0:T(2,128)} %copy.83.qn_ref, f32[8,1,128]{2,1,0:T(1,128)} %bitcast.182, f32[768,128]{1,0:T(8,128)} %get-tuple-element.171.cos_ref, ...), custom_call_target="tpu_custom_call" | custom-call | flops 4831838208 | bytes 18874368 | tf_op jit(solution)/shard_map/pallas_call | solution.py:241
  165.9 21.5 %shard_map.447 = (f32[768,3072]{1,0:T(8,128)}, f32[768,3072]{1,0:T(8,128)}, bf16[768,3072]{1,0:T(8,128)(2,1)}, bf16[768,3072]{1,0:T(8,128)(2,1)}, bf16[768,3072]{1,0:T(8,128)(2,1)}) custom-call(s32[8]{0:T(128)} %gather_fusion.1, s32[8]{0:T(128)} %gather_fusion, bf16[768,1024]{1,0:T(8,128)(2,1)} %get-tuple-element.54.x_ref, ...), custom_call_target="tpu_custom_call" | custom-call | flops 9663676416 | bytes 45613056 | tf_op jit(solution)/shard_map/pallas_call | solution.py:97
  187.4 14.6 %shard_map.448.x_ref = bf16[768,1024]{1,0:T(8,128)(2,1)} custom-call(bf16[768,1024]{1,0:T(8,128)(2,1)} %bitcast.129, bf16[768,2048]{1,0:T(8,128)(2,1)} %get-tuple-element.55.a_ref, bf16[768,3072]{1,0:T(8,128)(2,1)} %get-tuple-element.56.m_ref, bf16[8,640,1024]{2,1,0:T(8,128)(2,1)} %bitcast.132), custom_call_target="tpu_custom_call" | custom-call | flops 8053063680 | bytes 18350080 | tf_op jit(solution)/shard_map/pallas_call | solution.py:121
  207.3 74.3 %all-gather.10.cloned.1.call-done.w_ref.wg_ref.wu_ref.refs_1_ = bf16[1024,10240]{1,0:T(8,128)(2,1)} async-done(((bf16[128,10240]{1,0:T(8,128)(2,1)}), bf16[1024,10240]{1,0:T(8,128)(2,1)}) %all-gather.10.cloned.1.call-update) | async-done | bytes 20971536 | tf_op jit(solution)/shard_map/all_gather | solution.py:349
  281.6 21.9 %shard_map.452 = (f32[768,3072]{1,0:T(8,128)}, f32[768,3072]{1,0:T(8,128)}, bf16[768,3072]{1,0:T(8,128)(2,1)}, bf16[768,3072]{1,0:T(8,128)(2,1)}, bf16[768,3072]{1,0:T(8,128)(2,1)}) custom-call(s32[8]{0:T(128)} %gather_fusion.1, s32[8]{0:T(128)} %gather_fusion, bf16[768,1024]{1,0:T(8,128)(2,1)} %get-tuple-element.57.x_ref, ...), custom_call_target="tpu_custom_call" | custom-call | flops 9663676416 | bytes 45613056 | tf_op jit(solution)/shard_map/pallas_call | solution.py:97
  312.1 13.5 %shard_map.450.qkv_ref = f32[768,4096]{1,0:T(8,128)} custom-call(bf16[768,1024]{1,0:T(8,128)(2,1)} %get-tuple-element.57.x_ref, bf16[1024,10240]{1,0:T(8,128)(2,1)} %all-gather.10.cloned.1.call-done.w_ref.wg_ref.wu_ref.refs_1_), custom_call_target="tpu_custom_call" | custom-call | flops 6442450944 | bytes 20971520 | tf_op jit(solution)/shard_map/pallas_call | solution.py:72
  325.6 34.5 %shard_map.451 = (bf16[768,2048]{1,0:T(8,128)(2,1)}, bf16[768,2048]{1,0:T(8,128)(2,1)}) custom-call(s32[8]{0:T(128)} %gather_fusion.1, f32[768,4096]{1,0:T(8,128)} %shard_map.450.qkv_ref, f32[8,2,128]{2,1,0:T(2,128)} %copy.84.qn_ref, f32[8,1,128]{2,1,0:T(1,128)} %bitcast.184, f32[768,128]{1,0:T(8,128)} %get-tuple-element.171.cos_ref, ...), custom_call_target="tpu_custom_call" | custom-call | flops 4831838208 | bytes 18874368 | tf_op jit(solution)/shard_map/pallas_call | solution.py:241
  365.9 20.3 %shard_map.454 = (bf16[768,2048]{1,0:T(8,128)(2,1)}, bf16[768,3072]{1,0:T(8,128)(2,1)}, bf16[768,3072]{1,0:T(8,128)(2,1)}) custom-call(bf16[768,1024]{1,0:T(8,128)(2,1)} %bitcast.121, bf16[8,640,1024]{2,1,0:T(8,128)(2,1)} %bitcast.130, f32[768,3072]{1,0:T(8,128)} %get-tuple-element.60.g_ref, f32[768,3072]{1,0:T(8,128)} %get-tuple-element.61.u_ref), custom_call_target="tpu_custom_call" | custom-call | flops 8053063680 | bytes 41943040 | tf_op jit(solution)/shard_map/pallas_call | solution.py:148
  386.2 54.6 %shard_map.455 = (bf16[768,4096]{1,0:T(8,128)(2,1)}, f32[8,2,128]{2,1,0:T(2,128)}, f32[8,1,128]{2,1,0:T(1,128)}) custom-call(f32[768,4096]{1,0:T(8,128)} %shard_map.450.qkv_ref, f32[8,2,128]{2,1,0:T(2,128)} %copy.84.qn_ref, f32[8,1,128]{2,1,0:T(1,128)} %bitcast.185, f32[768,128]{1,0:T(8,128)} %get-tuple-element.171.cos_ref, ...), custom_call_target="tpu_custom_call" | custom-call | flops 12079595520 | bytes 22020096 | tf_op jit(solution)/shard_map/pallas_call | solution.py:294
  464.9 12.4 shard_map.457.refs_2_
  477.3 15.6 %shard_map.458 = f32[768,1024]{1,0:T(8,128)} custom-call(bf16[768,4096]{1,0:T(8,128)(2,1)} %get-tuple-element.63.refs_0_, bf16[1024,10240]{1,0:T(8,128)(2,1)} %all-gather.10.cloned.1.call-done.w_ref.wg_ref.wu_ref.refs_1_, f32[768,1024]{1,0:T(8,128)} %shard_map.457.refs_2_), custom_call_target="tpu_custom_call" | custom-call | flops 6442450944 | bytes 17825792 | tf_op jit(solution)/shard_map/pallas_call | solution.py:187
  505.5 20.3 %shard_map.459 = (bf16[768,2048]{1,0:T(8,128)(2,1)}, bf16[768,3072]{1,0:T(8,128)(2,1)}, bf16[768,3072]{1,0:T(8,128)(2,1)}) custom-call(bf16[768,1024]{1,0:T(8,128)(2,1)} %copy-done.2, bf16[8,640,1024]{2,1,0:T(8,128)(2,1)} %bitcast.133, f32[768,3072]{1,0:T(8,128)} %get-tuple-element.66.g_ref, f32[768,3072]{1,0:T(8,128)} %get-tuple-element.67.u_ref), custom_call_target="tpu_custom_call" | custom-call | flops 8053063680 | bytes 41943040 | tf_op jit(solution)/shard_map/pallas_call | solution.py:148
  525.8 54.3 %shard_map.460 = (bf16[768,4096]{1,0:T(8,128)(2,1)}, f32[8,2,128]{2,1,0:T(2,128)}, f32[8,1,128]{2,1,0:T(1,128)}) custom-call(f32[768,4096]{1,0:T(8,128)} %shard_map.445.qkv_ref, f32[8,2,128]{2,1,0:T(2,128)} %copy.83.qn_ref, f32[8,1,128]{2,1,0:T(1,128)} %bitcast.183, f32[768,128]{1,0:T(8,128)} %get-tuple-element.171.cos_ref, ...), custom_call_target="tpu_custom_call" | custom-call | flops 12079595520 | bytes 22020096 | tf_op jit(solution)/shard_map/pallas_call | solution.py:294
  603.8 12.4 shard_map.462.refs_2_
  616.3 15.3 %shard_map.463 = f32[768,1024]{1,0:T(8,128)} custom-call(bf16[768,4096]{1,0:T(8,128)(2,1)} %get-tuple-element.69.refs_0_, bf16[1024,10240]{1,0:T(8,128)(2,1)} %all-gather.8.cloned.1.call-done.w_ref.wg_ref.wu_ref.refs_1_, f32[768,1024]{1,0:T(8,128)} %shard_map.462.refs_2_), custom_call_target="tpu_custom_call" | custom-call | flops 6442450944 | bytes 17825792 | tf_op jit(solution)/shard_map/pallas_call | solution.py:187
  634.8 13.9 %shard_map.453 = bf16[768,1024]{1,0:T(8,128)(2,1)} custom-call(bf16[768,1024]{1,0:T(8,128)(2,1)} %shard_map.448.x_ref, bf16[768,2048]{1,0:T(8,128)(2,1)} %get-tuple-element.58.a_ref, bf16[768,3072]{1,0:T(8,128)(2,1)} %get-tuple-element.59.m_ref, bf16[8,640,1024]{2,1,0:T(8,128)(2,1)} %bitcast.131), custom_call_target="tpu_custom_call" | custom-call | flops 8053063680 | bytes 18350080 | tf_op jit(solution)/shard_map/pallas_call | solution.py:121
  735.8 18.8 %collective-permute-done.43 = f32[768,512]{0,1:T(8,128)S(1)} collective-permute-done((f32[768,512]{0,1:T(8,128)}, f32[768,512]{0,1:T(8,128)S(1)}, u32[]{:S(2)}, u32[]{:S(2)}) %collective-permute-start.43) | collective-permute-done | bytes 1572896 | tf_op jit(solution)/shard_map/ppermute | solution.py:322
  761.1 26.4 %collective-permute-done.19 = f32[768,512]{0,1:T(8,128)S(1)} collective-permute-done((f32[768,512]{0,1:T(8,128)}, f32[768,512]{0,1:T(8,128)S(1)}, u32[]{:S(2)}, u32[]{:S(2)}) %collective-permute-start.19) | collective-permute-done | bytes 1572896 | tf_op jit(solution)/shard_map/ppermute | solution.py:322
  798.0 14.3 %collective-permute-done.44 = f32[384,512]{0,1:T(8,128)S(1)} collective-permute-done((f32[384,512]{0,1:T(8,128)S(1)}, f32[384,512]{0,1:T(8,128)S(1)}, u32[]{:S(2)}, u32[]{:S(2)}) %collective-permute-start.44) | collective-permute-done | bytes 786464 | tf_op jit(solution)/shard_map/ppermute | solution.py:322
  839.2 36.9 %collective-permute-done.23 = f32[384,512]{0,1:T(8,128)S(1)} collective-permute-done((f32[384,512]{0,1:T(8,128)S(1)}, f32[384,512]{0,1:T(8,128)S(1)}, u32[]{:S(2)}, u32[]{:S(2)}) %collective-permute-start.23) | collective-permute-done | bytes 786464 | tf_op jit(solution)/shard_map/ppermute | solution.py:322
  892.0 30.5 %collective-permute-done.10 = f32[512,1024]{1,0:T(8,128)} collective-permute-done((f32[512,1024]{1,0:T(8,128)}, f32[512,1024]{1,0:T(8,128)}, u32[]{:S(2)}, u32[]{:S(2)}) %collective-permute-start.10) | collective-permute-done | bytes 2097184 | tf_op jit(solution)/shard_map/ppermute | solution.py:322
  951.8 19.6 %collective-permute-done.28 = f32[256,2048]{1,0:T(8,128)} collective-permute-done((f32[256,2048]{1,0:T(8,128)}, f32[256,2048]{1,0:T(8,128)}, u32[]{:S(2)}, u32[]{:S(2)}) %collective-permute-start.28) | collective-permute-done | bytes 2097184 | tf_op jit(solution)/shard_map/ppermute | solution.py:322
  985.4 30.9 %collective-permute-done.4 = f32[256,2048]{1,0:T(8,128)} collective-permute-done((f32[256,2048]{1,0:T(8,128)}, f32[256,2048]{1,0:T(8,128)}, u32[]{:S(2)}, u32[]{:S(2)}) %collective-permute-start.4) | collective-permute-done | bytes 2097184 | tf_op jit(solution)/shard_map/ppermute | solution.py:322
  1021.8 107.5 %collective-permute-done.29 = f32[128,2048]{1,0:T(8,128)S(1)} collective-permute-done((f32[128,2048]{1,0:T(8,128)S(1)}, f32[128,2048]{1,0:T(8,128)S(1)}, u32[]{:S(2)}, u32[]{:S(2)}) %collective-permute-start.29) | collective-permute-done | bytes 1048608 | tf_op jit(solution)/shard_map/ppermute | solution.py:322
  1132.2 20.4 %collective-permute-done.5 = f32[128,2048]{1,0:T(8,128)S(1)} collective-permute-done((f32[128,2048]{1,0:T(8,128)S(1)}, f32[128,2048]{1,0:T(8,128)S(1)}, u32[]{:S(2)}, u32[]{:S(2)}) %collective-permute-start.5) | collective-permute-done | bytes 1048608 | tf_op jit(solution)/shard_map/ppermute | solution.py:322
  1188.3 35.3 %collective-permute-done.16 = f32[256,3072]{1,0:T(8,128)S(1)} collective-permute-done((f32[256,3072]{1,0:T(8,128)S(1)}, f32[256,3072]{1,0:T(8,128)S(1)}, u32[]{:S(2)}, u32[]{:S(2)}) %collective-permute-start.16) | collective-permute-done | bytes 3145760 | tf_op jit(solution)/shard_map/ppermute | solution.py:322
  1224.1 24.4 %collective-permute-done.13 = f32[256,3072]{1,0:T(8,128)S(1)} collective-permute-done((f32[256,3072]{1,0:T(8,128)S(1)}, f32[256,3072]{1,0:T(8,128)S(1)}, u32[]{:S(2)}, u32[]{:S(2)}) %collective-permute-start.13) | collective-permute-done | bytes 3145760 | tf_op jit(solution)/shard_map/ppermute | solution.py:322
  1249.8 32.4 %collective-permute-done.41 = f32[128,3072]{1,0:T(8,128)S(1)} collective-permute-done((f32[128,3072]{1,0:T(8,128)S(1)}, f32[128,3072]{1,0:T(8,128)S(1)}, u32[]{:S(2)}, u32[]{:S(2)}) %collective-permute-start.41) | collective-permute-done | bytes 1572896 | tf_op jit(solution)/shard_map/ppermute | solution.py:322
  1287.9 22.1 %collective-permute-done.17 = f32[128,3072]{1,0:T(8,128)S(1)} collective-permute-done((f32[128,3072]{1,0:T(8,128)S(1)}, f32[128,3072]{1,0:T(8,128)S(1)}, u32[]{:S(2)}, u32[]{:S(2)}) %collective-permute-start.17) | collective-permute-done | bytes 1572896 | tf_op jit(solution)/shard_map/ppermute | solution.py:322
  (467 shorter events, 355.9 us)
Async XLA Ops:
  7.2 110.6 %all-gather.8.cloned.1.call-start = ((), (), s32[]{:S(2)}) async-start(), calls=%async_computation | async-start | bytes 23592960 | tf_op jit(solution)/shard_map/all_gather | solution.py:349
  12.9 174.5 %all-gather.12.cloned.1.call-start = ((), (), s32[]{:S(2)}) async-start(), calls=%async_computation.2 | async-start | bytes 11796480 | tf_op jit(solution)/shard_map/all_gather | solution.py:349
  15.3 266.3 %all-gather.10.cloned.1.call-start = ((), (), s32[]{:S(2)}) async-start(), calls=%async_computation.1 | async-start | bytes 23592960 | tf_op jit(solution)/shard_map/all_gather | solution.py:349
  18.7 347.2 %all-gather.14.cloned.1.call-start = ((), (), s32[]{:S(2)}) async-start(), calls=%async_computation.3 | async-start | bytes 11796480 | tf_op jit(solution)/shard_map/all_gather | solution.py:349
  308.4 373.3 %collective-permute-start.42 = (f32[1536,512]{0,1:T(8,128)}, f32[1536,512]{0,1:T(8,128)}, u32[]{:S(2)}, u32[]{:S(2)}) collective-permute-start(f32[1536,512]{0,1:T(8,128)} %fusion.50), channel_id=1, source_target_pairs={{0,1},{1,0},{2,3},{3,2},{4,5},{5,4},{6,7},{7,6}} | collective-permute-start | bytes 9437192 | tf_op jit(solution)/shard_map/ppermute | solution.py:322
  311.8 374.1 %collective-permute-start.45 = (f32[1536,512]{0,1:T(8,128)}, f32[1536,512]{0,1:T(8,128)}, u32[]{:S(2)}, u32[]{:S(2)}) collective-permute-start(f32[1536,512]{0,1:T(8,128)} %fusion.48), channel_id=1, source_target_pairs={{0,1},{1,0},{2,3},{3,2},{4,5},{5,4},{6,7},{7,6}} | collective-permute-start | bytes 9437192 | tf_op jit(solution)/shard_map/ppermute | solution.py:322
  365.4 338.9 %collective-permute-start.33 = (f32[1024,1024]{1,0:T(8,128)}, f32[1024,1024]{1,0:T(8,128)}, u32[]{:S(2)}, u32[]{:S(2)}) collective-permute-start(f32[1024,1024]{1,0:T(8,128)} %fusion.61), channel_id=1, source_target_pairs={{0,1},{1,0},{2,3},{3,2},{4,5},{5,4},{6,7},{7,6}} | collective-permute-start | bytes 12582920 | tf_op jit(solution)/shard_map/ppermute | solution.py:322
  496.8 162.5 %collective-permute-start.24 = (f32[4,512]{1,0:T(4,128)S(1)}, f32[4,512]{1,0:T(4,128)S(1)}, u32[]{:S(2)}, u32[]{:S(2)}) collective-permute-start(f32[4,512]{1,0:T(4,128)S(1)} %slice.688), channel_id=1, source_target_pairs={{0,1},{1,0},{2,3},{3,2},{4,5},{5,4},{6,7},{7,6}} | collective-permute-start | bytes 24584 | tf_op jit(solution)/shard_map/ppermute | solution.py:322
  505.2 182.7 %collective-permute-start.18 = (f32[1536,512]{0,1:T(8,128)}, f32[1536,512]{0,1:T(8,128)}, u32[]{:S(2)}, u32[]{:S(2)}) collective-permute-start(f32[1536,512]{0,1:T(8,128)} %fusion.54), channel_id=1, source_target_pairs={{0,1},{1,0},{2,3},{3,2},{4,5},{5,4},{6,7},{7,6}} | collective-permute-start | bytes 9437192 | tf_op jit(solution)/shard_map/ppermute | solution.py:322
  704.1 55.8 %collective-permute-start.9 = (f32[1024,1024]{1,0:T(8,128)}, f32[1024,1024]{1,0:T(8,128)S(1)}, u32[]{:S(2)}, u32[]{:S(2)}) collective-permute-start(f32[1024,1024]{1,0:T(8,128)} %fusion.63), channel_id=1, source_target_pairs={{0,1},{1,0},{2,3},{3,2},{4,5},{5,4},{6,7},{7,6}} | collective-permute-start | bytes 12582920 | tf_op jit(solution)/shard_map/ppermute | solution.py:322
  704.3 55.7 %collective-permute-start.6 = (f32[512,2048]{1,0:T(8,128)S(1)}, f32[512,2048]{1,0:T(8,128)}, u32[]{:S(2)}, u32[]{:S(2)}) collective-permute-start(f32[512,2048]{1,0:T(8,128)S(1)} %fusion.38), channel_id=1, source_target_pairs={{0,1},{1,0},{2,3},{3,2},{4,5},{5,4},{6,7},{7,6}} | collective-permute-start | bytes 12582920 | tf_op jit(solution)/shard_map/ppermute | solution.py:322
  727.3 60.2 %collective-permute-start.19 = (f32[768,512]{0,1:T(8,128)}, f32[768,512]{0,1:T(8,128)S(1)}, u32[]{:S(2)}, u32[]{:S(2)}) collective-permute-start(f32[768,512]{0,1:T(8,128)} %slice_add_fusion.30), channel_id=1, source_target_pairs={{0,2},{1,3},{2,0},{3,1},{4,6},{5,7},{6,4},{7,5}} | collective-permute-start | bytes 4718600 | tf_op jit(solution)/shard_map/ppermute | solution.py:322
  754.6 171.4 %collective-permute-start.39 = (f32[512,3072]{1,0:T(8,128)}, f32[512,3072]{1,0:T(8,128)}, u32[]{:S(2)}, u32[]{:S(2)}) collective-permute-start(f32[512,3072]{1,0:T(8,128)} %fusion.123), channel_id=1, source_target_pairs={{0,1},{1,0},{2,3},{3,2},{4,5},{5,4},{6,7},{7,6}} | collective-permute-start | bytes 18874376 | tf_op jit(solution)/shard_map/ppermute | solution.py:322
  760.0 175.7 %collective-permute-start.36 = (f32[512,3072]{1,0:T(8,128)}, f32[512,3072]{1,0:T(8,128)}, u32[]{:S(2)}, u32[]{:S(2)}) collective-permute-start(f32[512,3072]{1,0:T(8,128)} %fusion.126), channel_id=1, source_target_pairs={{0,1},{1,0},{2,3},{3,2},{4,5},{5,4},{6,7},{7,6}} | collective-permute-start | bytes 18874376 | tf_op jit(solution)/shard_map/ppermute | solution.py:322
  760.0 52.2 %collective-permute-start.44 = (f32[384,512]{0,1:T(8,128)S(1)}, f32[384,512]{0,1:T(8,128)S(1)}, u32[]{:S(2)}, u32[]{:S(2)}) collective-permute-start(f32[384,512]{0,1:T(8,128)S(1)} %slice_add_fusion.50), channel_id=1, source_target_pairs={{0,4},{1,5},{2,6},{3,7},{4,0},{5,1},{6,2},{7,3}} | collective-permute-start | bytes 2359304 | tf_op jit(solution)/shard_map/ppermute | solution.py:322
  796.8 146.3 %collective-permute-start.15 = (f32[512,3072]{1,0:T(8,128)}, f32[512,3072]{1,0:T(8,128)}, u32[]{:S(2)}, u32[]{:S(2)}) collective-permute-start(f32[512,3072]{1,0:T(8,128)} %fusion.129), channel_id=1, source_target_pairs={{0,1},{1,0},{2,3},{3,2},{4,5},{5,4},{6,7},{7,6}} | collective-permute-start | bytes 18874376 | tf_op jit(solution)/shard_map/ppermute | solution.py:322
  812.3 67.2 %collective-permute-start.34 = (f32[512,1024]{1,0:T(8,128)S(1)}, f32[512,1024]{1,0:T(8,128)S(1)}, u32[]{:S(2)}, u32[]{:S(2)}) collective-permute-start(f32[512,1024]{1,0:T(8,128)S(1)} %slice_add_fusion.8), channel_id=1, source_target_pairs={{0,2},{1,3},{2,0},{3,1},{4,6},{5,7},{6,4},{7,5}} | collective-permute-start | bytes 6291464 | tf_op jit(solution)/shard_map/ppermute | solution.py:322
  879.4 96.1 %collective-permute-start.12 = (f32[512,3072]{1,0:T(8,128)}, f32[512,3072]{1,0:T(8,128)}, u32[]{:S(2)}, u32[]{:S(2)}) collective-permute-start(f32[512,3072]{1,0:T(8,128)} %fusion.132), channel_id=1, source_target_pairs={{0,1},{1,0},{2,3},{3,2},{4,5},{5,4},{6,7},{7,6}} | collective-permute-start | bytes 18874376 | tf_op jit(solution)/shard_map/ppermute | solution.py:322
  922.5 48.8 %collective-permute-start.28 = (f32[256,2048]{1,0:T(8,128)}, f32[256,2048]{1,0:T(8,128)}, u32[]{:S(2)}, u32[]{:S(2)}) collective-permute-start(f32[256,2048]{1,0:T(8,128)} %slice_add_fusion.12), channel_id=1, source_target_pairs={{0,2},{1,3},{2,0},{3,1},{4,6},{5,7},{6,4},{7,5}} | collective-permute-start | bytes 6291464 | tf_op jit(solution)/shard_map/ppermute | solution.py:322
  935.6 80.7 %collective-permute-start.4 = (f32[256,2048]{1,0:T(8,128)}, f32[256,2048]{1,0:T(8,128)}, u32[]{:S(2)}, u32[]{:S(2)}) collective-permute-start(f32[256,2048]{1,0:T(8,128)} %slice_add_fusion.18), channel_id=1, source_target_pairs={{0,2},{1,3},{2,0},{3,1},{4,6},{5,7},{6,4},{7,5}} | collective-permute-start | bytes 6291464 | tf_op jit(solution)/shard_map/ppermute | solution.py:322
  943.2 76.6 %collective-permute-start.7 = (f32[256,2048]{1,0:T(8,128)}, f32[256,2048]{1,0:T(8,128)}, u32[]{:S(2)}, u32[]{:S(2)}) collective-permute-start(f32[256,2048]{1,0:T(8,128)} %slice_add_fusion.16), channel_id=1, source_target_pairs={{0,4},{1,5},{2,6},{3,7},{4,0},{5,1},{6,2},{7,3}} | collective-permute-start | bytes 6291464 | tf_op jit(solution)/shard_map/ppermute | solution.py:322
  971.4 212.2 %collective-permute-start.40 = (f32[256,3072]{1,0:T(8,128)S(1)}, f32[256,3072]{1,0:T(8,128)}, u32[]{:S(2)}, u32[]{:S(2)}) collective-permute-start(f32[256,3072]{1,0:T(8,128)S(1)} %slice_add_fusion), channel_id=1, source_target_pairs={{0,4},{1,5},{2,6},{3,7},{4,0},{5,1},{6,2},{7,3}} | collective-permute-start | bytes 9437192 | tf_op jit(solution)/shard_map/ppermute | solution.py:322
  974.7 210.8 %collective-permute-start.37 = (f32[256,3072]{1,0:T(8,128)S(1)}, f32[256,3072]{1,0:T(8,128)}, u32[]{:S(2)}, u32[]{:S(2)}) collective-permute-start(f32[256,3072]{1,0:T(8,128)S(1)} %slice_add_fusion.2), channel_id=1, source_target_pairs={{0,2},{1,3},{2,0},{3,1},{4,6},{5,7},{6,4},{7,5}} | collective-permute-start | bytes 9437192 | tf_op jit(solution)/shard_map/ppermute | solution.py:322
  975.6 186.1 %collective-permute-start.35 = (f32[256,1024]{1,0:T(8,128)S(1)}, f32[256,1024]{1,0:T(8,128)}, u32[]{:S(2)}, u32[]{:S(2)}) collective-permute-start(f32[256,1024]{1,0:T(8,128)S(1)} %slice_add_fusion.36), channel_id=1, source_target_pairs={{0,4},{1,5},{2,6},{3,7},{4,0},{5,1},{6,2},{7,3}} | collective-permute-start | bytes 3145736 | tf_op jit(solution)/shard_map/ppermute | solution.py:322
  1016.3 113.0 %collective-permute-start.29 = (f32[128,2048]{1,0:T(8,128)S(1)}, f32[128,2048]{1,0:T(8,128)S(1)}, u32[]{:S(2)}, u32[]{:S(2)}) collective-permute-start(f32[128,2048]{1,0:T(8,128)S(1)} %slice_add_fusion.40), channel_id=1, source_target_pairs={{0,4},{1,5},{2,6},{3,7},{4,0},{5,1},{6,2},{7,3}} | collective-permute-start | bytes 3145736 | tf_op jit(solution)/shard_map/ppermute | solution.py:322
  1019.8 111.9 %collective-permute-start.32 = (f32[128,2048]{1,0:T(8,128)S(1)}, f32[128,2048]{1,0:T(8,128)S(1)}, u32[]{:S(2)}, u32[]{:S(2)}) collective-permute-start(f32[128,2048]{1,0:T(8,128)S(1)} %slice_add_fusion.38), channel_id=1, source_target_pairs={{0,2},{1,3},{2,0},{3,1},{4,6},{5,7},{6,4},{7,5}} | collective-permute-start | bytes 3145736 | tf_op jit(solution)/shard_map/ppermute | solution.py:322
  1152.6 71.0 %collective-permute-start.16 = (f32[256,3072]{1,0:T(8,128)S(1)}, f32[256,3072]{1,0:T(8,128)S(1)}, u32[]{:S(2)}, u32[]{:S(2)}) collective-permute-start(f32[256,3072]{1,0:T(8,128)S(1)} %slice_add_fusion.4), channel_id=1, source_target_pairs={{0,4},{1,5},{2,6},{3,7},{4,0},{5,1},{6,2},{7,3}} | collective-permute-start | bytes 9437192 | tf_op jit(solution)/shard_map/ppermute | solution.py:322
  1162.7 85.8 %collective-permute-start.13 = (f32[256,3072]{1,0:T(8,128)S(1)}, f32[256,3072]{1,0:T(8,128)S(1)}, u32[]{:S(2)}, u32[]{:S(2)}) collective-permute-start(f32[256,3072]{1,0:T(8,128)S(1)} %copy-done.33), channel_id=1, source_target_pairs={{0,2},{1,3},{2,0},{3,1},{4,6},{5,7},{6,4},{7,5}} | collective-permute-start | bytes 9437192 | tf_op jit(solution)/shard_map/ppermute | solution.py:322
  1185.2 97.0 %collective-permute-start.41 = (f32[128,3072]{1,0:T(8,128)S(1)}, f32[128,3072]{1,0:T(8,128)S(1)}, u32[]{:S(2)}, u32[]{:S(2)}) collective-permute-start(f32[128,3072]{1,0:T(8,128)S(1)} %slice_add_fusion.24), channel_id=1, source_target_pairs={{0,2},{1,3},{2,0},{3,1},{4,6},{5,7},{6,4},{7,5}} | collective-permute-start | bytes 4718600 | tf_op jit(solution)/shard_map/ppermute | solution.py:322
  1187.2 97.9 %collective-permute-start.38 = (f32[128,3072]{1,0:T(8,128)S(1)}, f32[128,3072]{1,0:T(8,128)S(1)}, u32[]{:S(2)}, u32[]{:S(2)}) collective-permute-start(f32[128,3072]{1,0:T(8,128)S(1)} %slice_add_fusion.26), channel_id=1, source_target_pairs={{0,4},{1,5},{2,6},{3,7},{4,0},{5,1},{6,2},{7,3}} | collective-permute-start | bytes 4718600 | tf_op jit(solution)/shard_map/ppermute | solution.py:322
  1223.8 86.2 %collective-permute-start.17 = (f32[128,3072]{1,0:T(8,128)S(1)}, f32[128,3072]{1,0:T(8,128)S(1)}, u32[]{:S(2)}, u32[]{:S(2)}) collective-permute-start(f32[128,3072]{1,0:T(8,128)S(1)} %slice_add_fusion.32), channel_id=1, source_target_pairs={{0,2},{1,3},{2,0},{3,1},{4,6},{5,7},{6,4},{7,5}} | collective-permute-start | bytes 4718600 | tf_op jit(solution)/shard_map/ppermute | solution.py:322
  1248.7 62.8 %collective-permute-start.14 = (f32[128,3072]{1,0:T(8,128)S(1)}, f32[128,3072]{1,0:T(8,128)S(1)}, u32[]{:S(2)}, u32[]{:S(2)}) collective-permute-start(f32[128,3072]{1,0:T(8,128)S(1)} %slice_add_fusion.34), channel_id=1, source_target_pairs={{0,4},{1,5},{2,6},{3,7},{4,0},{5,1},{6,2},{7,3}} | collective-permute-start | bytes 4718600 | tf_op jit(solution)/shard_map/ppermute | solution.py:322
  (118 other events, 1824.2 us)
Sparse Core Ops, SparseCore 0:
  13.0 104.7 all-gather.7
  120.2 57.5 all-gather.11
  179.6 101.8 all-gather.9
  283.8 57.5 all-gather.13
